TPU v7x, 256 devices: a whole 4x4x8 slice. The times are simulated.
256 devices in a mesh: freq: 16 (over z, core), tm: 16 (over y, x).
Axes of the slice: x: 4, y: 4, z: 8, core: 2. Of those that a mesh axis runs over, the one named last changes fastest.
Arguments:
- band_state: float32 [2048, 16384], P('freq', 'tm'), may hold values from -2.5 to 2.5
- lower_rows: int32 [3, 2048], replicated, may hold values from 0 to 2047, as said below
- upper_rows: int32 [3, 2048], replicated, may hold values from 0 to 2047, as said below
- delays: int32 [3, 2048], replicated, may hold values from 0 to 1024, as said below
- counts: int32 [7], replicated, may hold values from 256 to 2048, as said below
Outputs:
- dedispersed: float32 [2048, 16384], P('freq', 'tm')
Inputs may be any that keep to these rules, and one draw needn't show every extreme that they name: `counts`: entry 8 - 8 / 2^k + b is the live row count of output sub-band b of iteration k; it lies between half and all of that sub-band's 2 * 2048 / 2^(3 - k) padded rows, and in every iteration some sub-band has all its rows live. With w = 2048 / 2^(3 - k), lower_rows[k, i] is a row of input sub-band 2 * floor(i / (2 * w)) whose position in that sub-band is below its live count (all w rows are live in iteration 0). With w = 2048 / 2^(3 - k), upper_rows[k, i] is a row of input sub-band 2 * floor(i / (2 * w)) + 1 whose position in that sub-band is below its live count (all w rows are live in iteration 0). delays[k, i] is at most 2048 / 2^(3 - k), and equals it at some row in every iteration.
All inputs are finite; a program needn't handle non-finite values.
Results may differ from a plain program's by a relative error of at most 0.0003.
Values sent between devices are 32-bit elements; how exact they have to be, the bound alone decides.
A program may use at most 64 MiB of HBM per device.

v0:
```python
import jax
import jax.numpy as jnp
from jax import lax
from jax.sharding import PartitionSpec as P

DMAX = 2048
ITERS = 3


def shifted_2(block, axis, distance):
    devices = range(lax.axis_size(axis))
    route = [(i - distance, i) for i in devices if i - distance in devices]
    return lax.ppermute(block, axis, route)


def delay_columns(extended, shifts, widest):
    row_count = extended.shape[0]
    for bit_index in range(widest.bit_length()):
        stride = 1 << bit_index
        shifted = jnp.concatenate(
            [jnp.zeros((row_count, stride), extended.dtype), extended[:, :-stride]], axis=1
        )
        extended = jnp.where((shifts >> bit_index & 1)[:, None] == 1, shifted, extended)
    return extended


def live_mask(global_rows, counts, width_out, offset, bands_out):
    band_index = global_rows // width_out
    band_counts = counts[offset : offset + bands_out]
    matches = band_index[:, None] == jnp.arange(bands_out, dtype=jnp.int32)[None, :]
    live_count = jnp.sum(jnp.where(matches, band_counts[None, :], 0), axis=1)
    return global_rows % width_out < live_count


def per_device(band_state, lower_rows, upper_rows, delays, counts):
    row_count, samples = band_state.shape
    freq_index = lax.axis_index("freq")
    first_row = freq_index * row_count
    global_rows = first_row + jnp.arange(row_count, dtype=jnp.int32)
    current = band_state
    for iteration in range(ITERS):
        width_in = DMAX >> ITERS - iteration
        width_out = 2 * width_in
        bands_out = DMAX // width_out
        offset = 2**ITERS - 2 ** (ITERS - iteration)
        lower_source = lax.dynamic_slice_in_dim(lower_rows[iteration], first_row, row_count)
        upper_source = lax.dynamic_slice_in_dim(upper_rows[iteration], first_row, row_count)
        own_delays = lax.dynamic_slice_in_dim(delays[iteration], first_row, row_count)
        gathered = lax.all_gather(current, "freq", axis=0, tiled=True)
        lower_values = jnp.take(gathered, lower_source, axis=0)
        upper_values = jnp.take(gathered, upper_source, axis=0)
        rim_columns = shifted_2(upper_values[:, samples - width_in :], "tm", 1)
        extended = jnp.concatenate([rim_columns, upper_values], axis=1)
        delayed = delay_columns(extended, own_delays, width_in)[:, width_in:]
        live_rows = live_mask(global_rows, counts, width_out, offset, bands_out)
        current = jnp.where(live_rows[:, None], lower_values + delayed, jnp.zeros_like(delayed))
    return current


def solution(mesh):
    return jax.shard_map(
        per_device,
        mesh=mesh,
        in_specs=(P("freq", "tm"), P(), P(), P(), P()),
        out_specs=P("freq", "tm"),
        check_vma=False,
    )
```

profile of v0, /device:TPU:5, one launch (start us, length us, event | category | flops | bytes accessed | tf_op | source)
XLA Modules:
  0.0 241.6 jit_solution(487976752341627834)
XLA Ops:
  6.5 0.7 all-gather.4.cloned.1.call-update
  7.3 0.9 fusion.24
  8.2 0.9 fusion.23
  9.1 0.9 fusion.25
  10.1 0.7 select_reduce_fusion
  10.8 57.5 %all-gather.4.cloned.1.call-done = f32[2048,1024]{1,0:T(8,128)} async-done(((f32[128,1024]{1,0:T(8,128)}), f32[2048,1024]{1,0:T(8,128)}) %all-gather.4.cloned.1.call-update) | async-done | bytes 8388624 | tf_op jit(solution)/shard_map/all_gather | solution.py:49
  68.4 4.4 %gather_fusion.1 = f32[128,1024]{1,0:T(8,128)S(1)} fusion(f32[2048,1024]{1,0:T(8,128)} %all-gather.4.cloned.1.call-done, s32[1024]{0:T(1024)S(1)} %pad_clamp_fusion.4), kind=kCustom, calls=%fused_computation.1.clone | custom fusion | bytes 1049088 | tf_op jit(solution)/shard_map/jit(_take)/gather | solution.py:51
  72.9 2.8 %collective-permute-start = (f32[128,256]{1,0:T(8,128)S(1)}, f32[128,256]{1,0:T(8,128)S(1)}, u32[]{:S(2)}, u32[]{:S(2)}) collective-permute-start(f32[128,256]{1,0:T(8,128)S(1)} %slice.200), channel_id=1, source_target_pairs={{0,1},{1,2},{2,3},{3,4},{4,5},{5,6},{6,7},{7,8},{8,9},{9,10},{10,1... | collective-permute-start | bytes 393224 | tf_op jit(solution)/shard_map/ppermute | solution.py:13
  75.8 4.4 %gather_fusion = f32[128,1024]{1,0:T(8,128)S(1)} fusion(f32[2048,1024]{1,0:T(8,128)} %all-gather.4.cloned.1.call-done, s32[1024]{0:T(1024)S(1)} %pad_clamp_fusion.5), kind=kCustom, calls=%fused_computation.clone | custom fusion | bytes 1049088 | tf_op jit(solution)/shard_map/jit(_take)/gather | solution.py:50
  80.3 0.3 fusion.5
  80.5 0.3 pad_select_fusion.23
  80.8 0.3 pad_select_fusion.22
  81.0 0.3 pad_select_fusion.21
  81.3 0.3 pad_select_fusion.20
  81.6 0.3 pad_select_fusion.19
  81.8 0.3 pad_select_fusion.18
  82.3 1.0 fusion.11
  83.6 54.5 %all-gather.6.cloned.1.call-done = f32[2048,1024]{1,0:T(8,128)} async-done(((f32[128,1024]{1,0:T(8,128)}), f32[2048,1024]{1,0:T(8,128)}) %all-gather.6.cloned.1.call-update) | async-done | bytes 8388624 | tf_op jit(solution)/shard_map/all_gather | solution.py:49
  138.1 4.4 %gather_fusion.3 = f32[128,1024]{1,0:T(8,128)S(1)} fusion(f32[2048,1024]{1,0:T(8,128)} %all-gather.6.cloned.1.call-done, s32[1024]{0:T(1024)S(1)} %pad_clamp_fusion.2), kind=kCustom, calls=%fused_computation.3.clone | custom fusion | bytes 1049088 | tf_op jit(solution)/shard_map/jit(_take)/gather | solution.py:51
  142.7 2.8 %collective-permute-start.1 = (f32[128,512]{1,0:T(8,128)S(1)}, f32[128,512]{1,0:T(8,128)S(1)}, u32[]{:S(2)}, u32[]{:S(2)}) collective-permute-start(f32[128,512]{1,0:T(8,128)S(1)} %slice.212), channel_id=1, source_target_pairs={{0,1},{1,2},{2,3},{3,4},{4,5},{5,6},{6,7},{7,8},{8,9},{9,10},{10,1... | collective-permute-start | bytes 786440 | tf_op jit(solution)/shard_map/ppermute | solution.py:13
  145.5 4.4 %gather_fusion.2 = f32[128,1024]{1,0:T(8,128)S(1)} fusion(f32[2048,1024]{1,0:T(8,128)} %all-gather.6.cloned.1.call-done, s32[1024]{0:T(1024)S(1)} %pad_clamp_fusion.3), kind=kCustom, calls=%fused_computation.2.clone | custom fusion | bytes 1049088 | tf_op jit(solution)/shard_map/jit(_take)/gather | solution.py:50
  150.0 2.2 collective-permute-done.1
  152.2 0.3 fusion.3
  152.5 0.3 pad_select_fusion.16
  152.8 0.3 pad_select_fusion.15
  153.1 0.3 pad_select_fusion.14
  153.4 0.3 pad_select_fusion.13
  153.7 0.3 pad_select_fusion.12
  154.0 0.3 pad_select_fusion.11
  154.7 1.0 fusion.9
  155.7 0.6 slice.141
  156.3 54.8 %all-gather.8.cloned.1.call-done = f32[2048,1024]{1,0:T(8,128)} async-done(((f32[128,1024]{1,0:T(8,128)}), f32[2048,1024]{1,0:T(8,128)}) %all-gather.8.cloned.1.call-update) | async-done | bytes 8388624 | tf_op jit(solution)/shard_map/all_gather | solution.py:49
  211.1 4.4 %gather_fusion.5 = f32[128,1024]{1,0:T(8,128)S(1)} fusion(f32[2048,1024]{1,0:T(8,128)} %all-gather.8.cloned.1.call-done, s32[1024]{0:T(1024)S(1)} %pad_clamp_fusion), kind=kCustom, calls=%fused_computation.5.clone | custom fusion | bytes 1049088 | tf_op jit(solution)/shard_map/jit(_take)/gather | solution.py:51
  215.6 2.8 %collective-permute-start.2 = (f32[128,1024]{1,0:T(8,128)S(1)}, f32[128,1024]{1,0:T(8,128)S(1)}, u32[]{:S(2)}, u32[]{:S(2)}) collective-permute-start(f32[128,1024]{1,0:T(8,128)S(1)} %broadcast_select_fusion), channel_id=1, source_target_pairs={{0,1},{1,2},{2,3},{3,4},{4,5},{5,6},{6,7},{7,8},{8,9},{9,10},{10,1... | collective-permute-start | bytes 1572872 | tf_op jit(solution)/shard_map/ppermute | solution.py:13
  218.4 0.6 fusion.13
  219.1 4.4 %gather_fusion.4 = f32[128,1024]{1,0:T(8,128)S(1)} fusion(f32[2048,1024]{1,0:T(8,128)} %all-gather.8.cloned.1.call-done, s32[1024]{0:T(1024)S(1)} %pad_clamp_fusion.1), kind=kCustom, calls=%fused_computation.4.clone | custom fusion | bytes 1049088 | tf_op jit(solution)/shard_map/jit(_take)/gather | solution.py:50
  223.6 7.2 %collective-permute-done.2 = f32[128,1024]{1,0:T(8,128)S(1)} collective-permute-done((f32[128,1024]{1,0:T(8,128)S(1)}, f32[128,1024]{1,0:T(8,128)S(1)}, u32[]{:S(2)}, u32[]{:S(2)}) %collective-permute-start.2) | collective-permute-done | bytes 524320 | tf_op jit(solution)/shard_map/ppermute | solution.py:13
  230.8 0.4 fusion.1
  231.2 0.4 pad_select_fusion.8
  231.5 0.4 pad_select_fusion.7
  231.9 0.4 pad_select_fusion.6
  232.2 0.4 pad_select_fusion.5
  232.6 0.4 pad_select_fusion.4
  232.9 0.4 pad_select_fusion.3
  233.4 0.2 pad_select_fusion.2
  233.6 0.2 pad_select_fusion.1
  233.9 0.2 pad_select_fusion
  234.1 1.0 fusion.7
  (49 shorter events, 1.8 us)
Async XLA Ops:
  6.5 61.8 %all-gather.4.cloned.1.call-start = ((), (), s32[]{:S(2)}) async-start(), calls=%async_computation | async-start | bytes 8912896 | tf_op jit(solution)/shard_map/all_gather | solution.py:49
  7.3 130.9 %all-gather.6.cloned.1.call-start = ((), (), s32[]{:S(2)}) async-start(), calls=%async_computation.1 | async-start | bytes 8912896 | tf_op jit(solution)/shard_map/all_gather | solution.py:49
  72.9 7.3 %collective-permute-start = (f32[128,256]{1,0:T(8,128)S(1)}, f32[128,256]{1,0:T(8,128)S(1)}, u32[]{:S(2)}, u32[]{:S(2)}) collective-permute-start(f32[128,256]{1,0:T(8,128)S(1)} %slice.200), channel_id=1, source_target_pairs={{0,1},{1,2},{2,3},{3,4},{4,5},{5,6},{6,7},{7,8},{8,9},{9,10},{10,1... | collective-permute-start | bytes 393224 | tf_op jit(solution)/shard_map/ppermute | solution.py:13
  80.8 2.6 %copy-start = (s32[7]{0:T(128)S(1)}, s32[7]{0:T(128)}, u32[]{:S(2)}) copy-start(s32[7]{0:T(128)} %param.11) | copy-start | bytes 88
  83.3 127.8 %all-gather.8.cloned.1.call-start = ((), (), s32[]{:S(2)}) async-start(), calls=%async_computation.2 | async-start | bytes 8912896 | tf_op jit(solution)/shard_map/all_gather | solution.py:49
  142.7 9.5 %collective-permute-start.1 = (f32[128,512]{1,0:T(8,128)S(1)}, f32[128,512]{1,0:T(8,128)S(1)}, u32[]{:S(2)}, u32[]{:S(2)}) collective-permute-start(f32[128,512]{1,0:T(8,128)S(1)} %slice.212), channel_id=1, source_target_pairs={{0,1},{1,2},{2,3},{3,4},{4,5},{5,6},{6,7},{7,8},{8,9},{9,10},{10,1... | collective-permute-start | bytes 786440 | tf_op jit(solution)/shard_map/ppermute | solution.py:13
  215.6 15.1 %collective-permute-start.2 = (f32[128,1024]{1,0:T(8,128)S(1)}, f32[128,1024]{1,0:T(8,128)S(1)}, u32[]{:S(2)}, u32[]{:S(2)}) collective-permute-start(f32[128,1024]{1,0:T(8,128)S(1)} %broadcast_select_fusion), channel_id=1, source_target_pairs={{0,1},{1,2},{2,3},{3,4},{4,5},{5,6},{6,7},{7,8},{8,9},{9,10},{10,1... | collective-permute-start | bytes 1572872 | tf_op jit(solution)/shard_map/ppermute | solution.py:13
Sparse Core Ops, SparseCore 0:
  9.2 59.1 all-gather.3
  83.4 54.6 all-gather.5
  155.8 55.2 all-gather.7
where the time goes:
time: 245 us; the launch traced here: 242 us
  waiting for transfers between devices  177 us (72%)
  local copies, waits for them, and re-layouts  30.4 us (12%)
  between operations  13.6 us (6%)
  other arithmetic  12.1 us (5%)
  starting transfers between devices  8.49 us (3%)
    all_gather x3, waiting for transfers between devices, per_device(): gathered = lax.all_gather(current, 'freq', axis=0, tiled=True)  167 us
    gather x3, local copies, waits for them, and re-layouts, per_device(): lower_values = jnp.take(gathered, lower_source, axis=0)  13.3 us
    gather x3, local copies, waits for them, and re-layouts, per_device(): upper_values = jnp.take(gathered, upper_source, axis=0)  13.3 us
    ppermute x3, waiting for transfers between devices, shifted_2(): return lax.ppermute(block, axis, route)  9.35 us
    ppermute x3, starting transfers between devices, shifted_2(): return lax.ppermute(block, axis, route)  8.41 us
    select_n x27, other arithmetic, delay_columns(): jnp.where((shifts >> bit_index & 1)[:, None] == 1, shifted, extended)  7.11 us
  transfers between devices with their start and end apart: 6, of which 5 were waited for; matrix products, arithmetic and copies ran while one was open for 8% of the time, Pallas kernels for 0%

commit v1 on v0

v1 whole, which is shorter than its diff:
```python
import jax
import jax.numpy as jnp
from jax import lax
from jax.experimental import pallas as pl
from jax.experimental.pallas import tpu as pltpu
from jax.sharding import PartitionSpec as P

DMAX = 2048
ITERS = 3
MESH = pl.DeviceIdType.MESH

CHIPS = 8
ROWS = 128
GROUPS = 32
TILES = 23
SPAN = TILES * 8
PAD, FAR, NEAR, OWN = 0, 1, 7, 15
UNIT = 32
HALF_UNITS = 64 // UNIT
ZERO_ROW = GROUPS * SPAN


def kernel(
    x, lower, upper, delays, counts, out,
    raw, select, delay, live, picks, sent, landed, result,
    local_sem, table_sem, near_sem, far_sem, own_sem, history_sem, send_sem, recv_sem, out_sem,
):
    freq = lax.axis_index("freq")
    tm = lax.axis_index("tm")
    tm_count = lax.axis_size("tm")
    z = lax.div(freq, 2)
    core = lax.rem(freq, 2)
    bits = [lax.rem(z, 2), lax.rem(lax.div(z, 2), 2), lax.div(z, 4)]
    partner = freq + 1 - 2 * core
    freq_up = lax.rem(freq + 2, 16)
    freq_down = lax.rem(freq + 14, 16)
    ring = (freq_up, freq_down)
    flat = raw.reshape((GROUPS + 1) * SPAN, 128)
    mine = pl.ds(core * 16, 16)
    theirs = pl.ds(16 - core * 16, 16)

    own = pltpu.make_async_copy(x, raw.at[mine, pl.ds(OWN * 8, 64), :], local_sem)
    own.start()
    tables = [
        pltpu.make_async_copy(source, target, table_sem.at[n])
        for n, (source, target) in enumerate(
            ((lower, select.at[0]), (upper, select.at[1]), (delays, delay), (counts, live))
        )
    ]
    for table in tables:
        table.start()

    barrier = pltpu.get_barrier_semaphore()
    peers = [
        {"freq": partner}, {"freq": freq_up}, {"freq": freq_down},
        {"tm": lax.rem(tm + 1, tm_count)}, {"tm": lax.rem(tm + tm_count - 1, tm_count)},
        {"tm": lax.rem(tm + 2, tm_count)}, {"tm": lax.rem(tm + tm_count - 2, tm_count)},
    ]
    for peer in peers:
        pl.semaphore_signal(barrier, inc=1, device_id=peer, device_id_type=MESH)
    pl.semaphore_wait(barrier, len(peers))

    own.wait()

    def remote(source, target, send, recv, device):
        return pltpu.make_async_remote_copy(
            src_ref=source, dst_ref=target, send_sem=send, recv_sem=recv,
            device_id=device, device_id_type=MESH,
        )

    near = remote(
        raw.at[mine, pl.ds(OWN * 8, 64), :], raw.at[mine, pl.ds(NEAR * 8, 64), :],
        near_sem.at[0], near_sem.at[1], {"tm": lax.rem(tm + 1, tm_count)},
    )
    far = remote(
        raw.at[mine, pl.ds((OWN + 2) * 8, 48), :], raw.at[mine, pl.ds(FAR * 8, 48), :],
        far_sem.at[0], far_sem.at[1], {"tm": lax.rem(tm + 2, tm_count)},
    )
    to_partner = remote(
        raw.at[mine, pl.ds(OWN * 8, 64), :], raw.at[mine, pl.ds(OWN * 8, 64), :],
        own_sem.at[0], own_sem.at[1], {"freq": partner},
    )
    near_across = remote(
        raw.at[mine, pl.ds(NEAR * 8, 64), :], raw.at[mine, pl.ds(NEAR * 8, 64), :],
        history_sem.at[0], history_sem.at[1], {"freq": partner},
    )
    far_across = remote(
        raw.at[mine, pl.ds(FAR * 8, 48), :], raw.at[mine, pl.ds(FAR * 8, 48), :],
        history_sem.at[2], history_sem.at[3], {"freq": partner},
    )

    @pl.when(tm < tm_count - 1)
    def _():
        near.start()

    @pl.when(tm < tm_count - 2)
    def _():
        far.start()

    to_partner.start()

    def clear(first, count):
        def body(g, carry):
            raw[g, pl.ds(first * 8, count * 8), :] = jnp.zeros((count * 8, 128), jnp.float32)
            return carry
        lax.fori_loop(0, GROUPS, body, 0)

    raw[GROUPS, :, :] = jnp.zeros((SPAN, 128), jnp.float32)

    @pl.when(tm == 0)
    def _():
        clear(NEAR, 8)

    @pl.when(tm <= 1)
    def _():
        clear(FAR, 6)

    for table in tables:
        table.wait()

    def pick(row, slot):
        late = delay[2, row] * bits[2]
        top = select[bits[2], 2, row]
        late += delay[1, top] * bits[1]
        middle = select[bits[1], 1, top]
        late += delay[0, middle] * bits[0]
        bottom = select[bits[0], 0, middle] & 255
        alive = ((top & 1023) < live[4 + (top >> 10)]) & ((middle & 511) < live[middle >> 9])
        start = (bottom >> 3) * SPAN + (bottom & 7) + OWN * 8 - (late >> 7) * 8
        start = jnp.where(alive, start, ZERO_ROW + OWN * 8)
        picks[slot] = start * 128 + (late & 127)

    for offset in (4, 3, 5, 2, 6, 1, 7, 0):
        base = lax.rem(z + offset, CHIPS) * 256 + core * ROWS

        def body(step, carry, base=base, offset=offset):
            for k in range(8):
                pick(base + step * 8 + k, offset * ROWS + step * 8 + k)
            return carry

        lax.fori_loop(0, ROWS // 8, body, 0)

    @pl.when(tm > 0)
    def _():
        near.wait_recv()
        near_across.start()

    @pl.when(tm > 1)
    def _():
        far.wait_recv()
        far_across.start()

    to_partner.wait_recv()

    @pl.when(tm > 0)
    def _():
        near_across.wait_recv()

    @pl.when(tm > 1)
    def _():
        far_across.wait_recv()

    lanes = lax.broadcasted_iota(jnp.int32, (8, 128), 1)

    def contribution(slot):
        packed = picks[slot]
        start = packed >> 7
        shift = packed & 127
        same = flat[pl.ds(start, 8, stride=8), :]
        before = flat[pl.ds(start - 8, 8, stride=8), :]
        return pltpu.roll(jnp.where(lanes < 128 - shift, same, before), shift, 1)

    def message(direction, step, half, unit):
        return (direction * 4 + step) * 2 * HALF_UNITS + half * HALF_UNITS + unit

    def copy_of(direction, step, half, unit):
        index = message(direction, step, half, unit)
        return remote(
            sent.at[index], landed.at[index], send_sem.at[index], recv_sem.at[index],
            {"freq": ring[direction]},
        )

    def add_and_send(direction, step, half, unit):
        index = message(direction, step, half, unit)
        offset = 4 - step if direction == 0 else 4 + step
        first_slot = offset * ROWS + half * 64 + unit * UNIT
        fresh = step == 0 or (step == 1 and half != direction)
        if not fresh:
            copy_of(direction, step - 1, half, unit).wait_recv()
        previous = message(direction, step - 1, half, unit)

        def body(i, carry):
            for k in range(8):
                row = i * 8 + k
                value = contribution(first_slot + row)
                at = pl.ds(pl.multiple_of(row * 8, 8), 8)
                if not fresh:
                    value = value + landed[previous, at, :]
                sent[index, at, :] = value
            return carry

        lax.fori_loop(0, UNIT // 8, body, 0)
        copy_of(direction, step, half, unit).start()

    messages = []
    for step in range(4):
        for turn in range(2):
            if step == 0 and turn == 0:
                continue
            for unit in range(HALF_UNITS):
                for direction in range(2):
                    half = direction if turn == 1 else 1 - direction
                    messages.append((direction, step, half, unit))
    for entry in messages:
        add_and_send(*entry)

    first_row = freq * ROWS
    finished = []
    for half in range(2):
        for unit in range(HALF_UNITS):
            incoming = []
            for direction in range(2):
                copy_of(direction, 3, half, unit).wait_recv()
                incoming.append(message(direction, 3, half, unit))

            def body(i, carry, half=half, unit=unit, incoming=incoming):
                for k in range(8):
                    row = i * 8 + k
                    local = half * 64 + unit * UNIT + row
                    at = pl.ds(pl.multiple_of(row * 8, 8), 8)
                    value = contribution(local) + landed[incoming[0], at, :] + landed[incoming[1], at, :]
                    alive = first_row + local < live[6]
                    value = jnp.where(alive, value, jnp.zeros_like(value))
                    place = (half * 64 + unit * UNIT) * 8 + i * 64 + k
                    result[pl.ds(place, 8, stride=8), :] = value
                return carry

            lax.fori_loop(0, UNIT // 8, body, 0)
            index = half * HALF_UNITS + unit
            rows = pl.ds(index * UNIT * 8, UNIT * 8)
            write = pltpu.make_async_copy(result.at[rows, :], out.at[rows, :], out_sem.at[index])
            write.start()
            finished.append(write)

    @pl.when(tm < tm_count - 1)
    def _():
        near.wait_send()

    @pl.when(tm < tm_count - 2)
    def _():
        far.wait_send()

    to_partner.wait_send()

    @pl.when(tm > 0)
    def _():
        near_across.wait_send()

    @pl.when(tm > 1)
    def _():
        far_across.wait_send()

    for entry in messages:
        copy_of(*entry).wait_send()
    for write in finished:
        write.wait()


def per_device(band_state, lower_rows, upper_rows, delays, counts):
    tiles = band_state.reshape(16, 8, 8, 128).transpose(0, 2, 1, 3).reshape(16, 64, 128)
    message_count = 2 * 4 * 2 * HALF_UNITS
    dma = pltpu.SemaphoreType.DMA
    out = pl.pallas_call(
        kernel,
        out_shape=jax.ShapeDtypeStruct((1024, 128), jnp.float32),
        in_specs=[pl.BlockSpec(memory_space=pl.ANY)] * 5,
        out_specs=pl.BlockSpec(memory_space=pl.ANY),
        scratch_shapes=[
            pltpu.VMEM((GROUPS + 1, SPAN, 128), jnp.float32),
            pltpu.SMEM((2, ITERS, DMAX), jnp.int32),
            pltpu.SMEM((ITERS, DMAX), jnp.int32),
            pltpu.SMEM((7,), jnp.int32),
            pltpu.SMEM((CHIPS * ROWS,), jnp.int32),
            pltpu.VMEM((message_count, UNIT * 8, 128), jnp.float32),
            pltpu.VMEM((message_count, UNIT * 8, 128), jnp.float32),
            pltpu.VMEM((1024, 128), jnp.float32),
            dma,
            dma((4,)),
            dma((2,)),
            dma((2,)),
            dma((2,)),
            dma((4,)),
            dma((message_count,)),
            dma((message_count,)),
            dma((2 * HALF_UNITS,)),
        ],
        compiler_params=pltpu.CompilerParams(collective_id=0, has_side_effects=True, vmem_limit_bytes=40 << 20),
    )(tiles, lower_rows, upper_rows, delays, counts)
    return out.reshape(16, 8, 8, 128).transpose(0, 2, 1, 3).reshape(ROWS, 1024)


def solution(mesh):
    return jax.shard_map(
        per_device,
        mesh=mesh,
        in_specs=(P("freq", "tm"), P(), P(), P(), P()),
        out_specs=P("freq", "tm"),
        check_vma=False,
    )
```

time: 245 us -> 81 us (0.33); the launches traced: 242 us -> 80.6 us
  waiting for transfers between devices: 177 us -> 0 us
  Pallas kernels: 0 us -> 75.9 us
  local copies, waits for them, and re-layouts: 30.4 us -> 4.76 us
  between operations: 13.6 us -> 0.01 us
  other arithmetic: 12.1 us -> 0 us
  starting transfers between devices: 8.49 us -> 0 us
    all_gather x3 -> x0, waiting for transfers between devices: 167 us -> none  [per_device(): gathered = lax.all_gather(current, 'freq', axis=0, tiled=True)]
    pallas_call x0 -> x1, Pallas kernels: none -> 75.9 us  [per_device(): pl.pallas_call(kernel, out_shape=jax.ShapeDtypeStruct((1024, 128), jnp.fl...]
    gather x6 -> x0, local copies, waits for them, and re-layouts: 26.5 us -> none  [the longest x3 13.3 us: per_device(): lower_values = jnp.take(gathered, lower_source, axis=0)]
    select_n x35 -> x0, other arithmetic: 10.3 us -> none  [the longest x27 7.11 us: delay_columns(): jnp.where((shifts >> bit_index & 1)[:, None] == 1, shifted, extended)]
    ppermute x3 -> x0, waiting for transfers between devices: 9.35 us -> none  [shifted_2(): return lax.ppermute(block, axis, route)]
    ppermute x3 -> x0, starting transfers between devices: 8.41 us -> none  [shifted_2(): return lax.ppermute(block, axis, route)]
    unnamed x2 -> x11, local copies, waits for them, and re-layouts: 0.01 us -> 4.76 us
    slice x16 -> x0, local copies, waits for them, and re-layouts: 3.84 us -> none  [the longest x1 0.9 us: per_device(): delays[iteration]]
  transfers between devices with their start and end apart: 6 -> 0, of which waited for: 5 -> 0; matrix products, arithmetic and copies ran while one was open for 8% -> 0% of each run, Pallas kernels for 0% -> 0%
where the time goes in v1:
time: 81 us; the launch traced here: 80.6 us
  Pallas kernels  75.9 us (94%)
  local copies, waits for them, and re-layouts  4.76 us (6%)
    pallas_call x1, Pallas kernels, per_device(): pl.pallas_call(kernel, out_shape=jax.ShapeDtypeStruct((1024, 128), jnp.fl...  75.9 us
    unnamed x11, local copies, waits for them, and re-layouts  4.76 us

profile of v1, /device:TPU:5, one launch (start us, length us, event | category | flops | bytes accessed | tf_op | source)
XLA Modules:
  0.0 80.6 jit_solution(648162088352144560)
XLA Ops:
  0.0 0.0 copy-start.4
  0.0 0.7 copy-done.4
  0.7 0.0 copy-start
  0.7 1.0 %copy-done = f32[128,1024]{1,0:T(8,128)S(1)} copy-done((f32[128,1024]{1,0:T(8,128)S(1)}, f32[128,1024]{1,0:T(8,128)}, u32[]{:S(2)}) %copy-start) | copy-done | bytes 524312
  1.7 0.0 copy-start.1
  1.7 0.8 copy-done.1
  2.5 0.0 copy-start.2
  2.5 0.8 copy-done.2
  3.2 0.0 copy-start.3
  3.2 0.8 copy-done.3
  4.0 75.9 %shard_map.55 = f32[1024,128]{1,0:T(8,128)S(1)} custom-call(f32[16,64,128]{2,1,0:T(8,128)S(1)} %bitcast.11, s32[3,2048]{1,0:T(4,128)S(1)} %copy-done.1, s32[3,2048]{1,0:T(4,128)S(1)} %copy-done.2, s32[3,2048]{1,0:T(4,128)S(1)} %copy-done.3, s32[7]{0:T(128)S(1)} %copy-done.4), custom_call_target="tpu_custom_call" | custom-call | tf_op jit(solution)/shard_map/pallas_call | solution.py:273
  79.8 0.8 copy.7
Async XLA Ops:
  0.0 0.7 copy-start.4
  0.7 1.0 %copy-start = (f32[128,1024]{1,0:T(8,128)S(1)}, f32[128,1024]{1,0:T(8,128)}, u32[]{:S(2)}) copy-start(f32[128,1024]{1,0:T(8,128)} %param.5) | copy-start | bytes 1572868
  1.7 0.8 copy-start.1
  2.5 0.8 copy-start.2
  3.2 0.8 copy-start.3

commit v2 on v1

--- a/solution.py
+++ b/solution.py
@@ -22,8 +22,8 @@
 
 def kernel(
     x, lower, upper, delays, counts, out,
-    raw, select, delay, live, picks, sent, landed, result,
-    local_sem, table_sem, near_sem, far_sem, own_sem, history_sem, send_sem, recv_sem, out_sem,
+    raw, lower_table, upper_table, delay_table, live, packed, picks, sent, landed,
+    local_sem, table_sem, near_sem, far_sem, own_sem, history_sem, send_sem, recv_sem,
 ):
     freq = lax.axis_index("freq")
     tm = lax.axis_index("tm")
@@ -44,7 +44,7 @@
     tables = [
         pltpu.make_async_copy(source, target, table_sem.at[n])
         for n, (source, target) in enumerate(
-            ((lower, select.at[0]), (upper, select.at[1]), (delays, delay), (counts, live))
+            ((lower, lower_table), (upper, upper_table), (delays, delay_table), (counts, live))
         )
     ]
     for table in tables:
@@ -118,27 +118,42 @@
     for table in tables:
         table.wait()
 
-    def pick(row, slot):
-        late = delay[2, row] * bits[2]
-        top = select[bits[2], 2, row]
-        late += delay[1, top] * bits[1]
-        middle = select[bits[1], 1, top]
-        late += delay[0, middle] * bits[0]
-        bottom = select[bits[0], 0, middle] & 255
-        alive = ((top & 1023) < live[4 + (top >> 10)]) & ((middle & 511) < live[middle >> 9])
-        start = (bottom >> 3) * SPAN + (bottom & 7) + OWN * 8 - (late >> 7) * 8
-        start = jnp.where(alive, start, ZERO_ROW + OWN * 8)
-        picks[slot] = start * 128 + (late & 127)
-
-    for offset in (4, 3, 5, 2, 6, 1, 7, 0):
-        base = lax.rem(z + offset, CHIPS) * 256 + core * ROWS
-
-        def body(step, carry, base=base, offset=offset):
-            for k in range(8):
-                pick(base + step * 8 + k, offset * ROWS + step * 8 + k)
-            return carry
-
-        lax.fori_loop(0, ROWS // 8, body, 0)
+    def entries(k, block):
+        at = (pl.ds(k, 1), pl.ds(block, 128))
+        row = jnp.where(bits[k] == 1, upper_table[at], lower_table[at])
+        return row * 2048 + delay_table[at] * bits[k]
+
+    def look_up(k, index):
+        found = jnp.zeros((8, 128), jnp.int32)
+        for block in range(DMAX // 128):
+            table = jnp.broadcast_to(entries(k, block * 128), (8, 128))
+            here = jnp.take_along_axis(table, index & 127, axis=1)
+            found = jnp.where(index >> 7 == block, here, found)
+        return found
+
+    def is_live(k, index):
+        bands = 4 >> k
+        width = DMAX // bands
+        first = 8 - (8 >> k)
+        count = jnp.full((8, 128), live[first], jnp.int32)
+        for band in range(1, bands):
+            count = jnp.where(index // width == band, live[first + band], count)
+        return (index & (width - 1)) < count
+
+    for offset in range(CHIPS):
+        block = lax.rem(z + offset, CHIPS) * 256 + core * ROWS
+        packed[pl.ds(offset, 1), :] = entries(2, pl.multiple_of(block, 128))
+    top = packed[...]
+    middle = look_up(1, top >> 11)
+    bottom = look_up(0, middle >> 11)
+    late = (top & 2047) + (middle & 2047) + (bottom & 2047)
+    row = (bottom >> 11) & 255
+    start = (row >> 3) * SPAN + (row & 7) + OWN * 8 - (late >> 7) * 8
+    start = jnp.where(is_live(1, top >> 11) & is_live(0, middle >> 11), start, ZERO_ROW + OWN * 8)
+    packed[...] = start * 128 + (late & 127)
+    to_scalar = pltpu.make_async_copy(packed, picks, table_sem.at[0])
+    to_scalar.start()
+    to_scalar.wait()
 
     @pl.when(tm > 0)
     def _():
@@ -162,10 +177,10 @@
 
     lanes = lax.broadcasted_iota(jnp.int32, (8, 128), 1)
 
-    def contribution(slot):
-        packed = picks[slot]
-        start = packed >> 7
-        shift = packed & 127
+    def contribution(offset, row):
+        entry = picks[offset, row]
+        start = entry >> 7
+        shift = entry & 127
         same = flat[pl.ds(start, 8, stride=8), :]
         before = flat[pl.ds(start - 8, 8, stride=8), :]
         return pltpu.roll(jnp.where(lanes < 128 - shift, same, before), shift, 1)
@@ -183,7 +198,7 @@
     def add_and_send(direction, step, half, unit):
         index = message(direction, step, half, unit)
         offset = 4 - step if direction == 0 else 4 + step
-        first_slot = offset * ROWS + half * 64 + unit * UNIT
+        first_row = half * 64 + unit * UNIT
         fresh = step == 0 or (step == 1 and half != direction)
         if not fresh:
             copy_of(direction, step - 1, half, unit).wait_recv()
@@ -192,7 +207,7 @@
         def body(i, carry):
             for k in range(8):
                 row = i * 8 + k
-                value = contribution(first_slot + row)
+                value = contribution(offset, first_row + row)
                 at = pl.ds(pl.multiple_of(row * 8, 8), 8)
                 if not fresh:
                     value = value + landed[previous, at, :]
@@ -215,7 +230,6 @@
         add_and_send(*entry)
 
     first_row = freq * ROWS
-    finished = []
     for half in range(2):
         for unit in range(HALF_UNITS):
             incoming = []
@@ -228,19 +242,14 @@
                     row = i * 8 + k
                     local = half * 64 + unit * UNIT + row
                     at = pl.ds(pl.multiple_of(row * 8, 8), 8)
-                    value = contribution(local) + landed[incoming[0], at, :] + landed[incoming[1], at, :]
+                    value = contribution(0, local) + landed[incoming[0], at, :] + landed[incoming[1], at, :]
                     alive = first_row + local < live[6]
                     value = jnp.where(alive, value, jnp.zeros_like(value))
                     place = (half * 64 + unit * UNIT) * 8 + i * 64 + k
-                    result[pl.ds(place, 8, stride=8), :] = value
+                    out[pl.ds(place, 8, stride=8), :] = value
                 return carry
 
             lax.fori_loop(0, UNIT // 8, body, 0)
-            index = half * HALF_UNITS + unit
-            rows = pl.ds(index * UNIT * 8, UNIT * 8)
-            write = pltpu.make_async_copy(result.at[rows, :], out.at[rows, :], out_sem.at[index])
-            write.start()
-            finished.append(write)
 
     @pl.when(tm < tm_count - 1)
     def _():
@@ -262,8 +271,6 @@
 
     for entry in messages:
         copy_of(*entry).wait_send()
-    for write in finished:
-        write.wait()
 
 
 def per_device(band_state, lower_rows, upper_rows, delays, counts):
@@ -273,17 +280,18 @@
     out = pl.pallas_call(
         kernel,
         out_shape=jax.ShapeDtypeStruct((1024, 128), jnp.float32),
-        in_specs=[pl.BlockSpec(memory_space=pl.ANY)] * 5,
-        out_specs=pl.BlockSpec(memory_space=pl.ANY),
+        in_specs=[pl.BlockSpec(memory_space=pltpu.HBM)] * 5,
+        out_specs=pl.BlockSpec(memory_space=pltpu.VMEM),
         scratch_shapes=[
             pltpu.VMEM((GROUPS + 1, SPAN, 128), jnp.float32),
-            pltpu.SMEM((2, ITERS, DMAX), jnp.int32),
-            pltpu.SMEM((ITERS, DMAX), jnp.int32),
+            pltpu.VMEM((ITERS, DMAX), jnp.int32),
+            pltpu.VMEM((ITERS, DMAX), jnp.int32),
+            pltpu.VMEM((ITERS, DMAX), jnp.int32),
             pltpu.SMEM((7,), jnp.int32),
-            pltpu.SMEM((CHIPS * ROWS,), jnp.int32),
+            pltpu.VMEM((CHIPS, ROWS), jnp.int32),
+            pltpu.SMEM((CHIPS, ROWS), jnp.int32),
             pltpu.VMEM((message_count, UNIT * 8, 128), jnp.float32),
             pltpu.VMEM((message_count, UNIT * 8, 128), jnp.float32),
-            pltpu.VMEM((1024, 128), jnp.float32),
             dma,
             dma((4,)),
             dma((2,)),
@@ -292,10 +300,9 @@
             dma((4,)),
             dma((message_count,)),
             dma((message_count,)),
-            dma((2 * HALF_UNITS,)),
         ],
         compiler_params=pltpu.CompilerParams(collective_id=0, has_side_effects=True, vmem_limit_bytes=40 << 20),
-    )(tiles, lower_rows, upper_rows, delays, counts)
+    )(*(pltpu.with_memory_space_constraint(a, pltpu.HBM) for a in (tiles, lower_rows, upper_rows, delays, counts)))
     return out.reshape(16, 8, 8, 128).transpose(0, 2, 1, 3).reshape(ROWS, 1024)
 
 

time: 81 us -> 76 us (0.938)
  local copies, waits for them, and re-layouts: 4.76 us -> 0.8 us
    unnamed x11 -> x1, local copies, waits for them, and re-layouts: 4.76 us -> 0.8 us
where the time goes in v2:
time: 76 us
  Pallas kernels  75.2 us (99%)
  local copies, waits for them, and re-layouts  0.8 us (1%)
    pallas_call x1, Pallas kernels, per_device(): pl.pallas_call(kernel, out_shape=jax.ShapeDtypeStruct((1024, 128), jnp.fl...  75.2 us

profile of v2, /device:TPU:5, one launch (start us, length us, event | category | flops | bytes accessed | tf_op | source)
XLA Modules:
  0.0 76.0 jit_solution(11494091315824577385)
XLA Ops:
  0.0 75.2 %shard_map.55 = f32[1024,128]{1,0:T(8,128)S(1)} custom-call(f32[16,64,128]{2,1,0:T(8,128)} %bitcast.11, s32[3,2048]{1,0:T(4,128)} %lower.1, s32[3,2048]{1,0:T(4,128)} %upper.1, s32[3,2048]{1,0:T(4,128)} %delays.1, s32[7]{0:T(128)} %counts.1), custom_call_target="tpu_custom_call" | custom-call | tf_op jit(solution)/shard_map/pallas_call | solution.py:280
  75.2 0.8 %copy.7 = f32[128,1024]{1,0:T(8,128)} copy(f32[128,1024]{1,0:T(8,128)S(1)} %bitcast.10) | data formatting | bytes 1048576

commit v3 on v2

v3 whole, which is shorter than its diff:
```python
import jax
import jax.numpy as jnp
from jax import lax
from jax.experimental import pallas as pl
from jax.experimental.pallas import tpu as pltpu
from jax.sharding import PartitionSpec as P

DMAX = 2048
ITERS = 3
MESH = pl.DeviceIdType.MESH

CHIPS = 8
ROWS = 128
GROUPS = 32
TILES = 23
SPAN = TILES * 8
SET = (GROUPS + 1) * SPAN
HERE = 11
SKEW = 4
PHASES = 2
WIDTH = 8 // PHASES
UNIT = 32
HALF_UNITS = 64 // UNIT
ZERO_ROW = GROUPS * SPAN

EARLY = SKEW + 8 - WIDTH - 14
FETCHES = [[(-1, 8 + EARLY, -EARLY), (1, 0, SKEW)]]
for phase in range(1, PHASES):
    last = EARLY - (phase - 1) * WIDTH
    first = last - WIDTH
    pieces = []
    if last > -8:
        pieces.append((-1, 8 + max(first, -8), last - max(first, -8)))
    if first < -8:
        pieces.append((-2, 16 + first, min(last, -8) - first))
    FETCHES.append(pieces)
LATE = [(phase, *piece) for phase in range(1, PHASES) for piece in FETCHES[phase]]


def kernel(
    x, lower, upper, delays, counts, out,
    raw, lower_table, upper_table, delay_table, live, packed, picks, sent, landed, late, shipped, received,
    local_sem, table_sem, own_sem, early_sem, late_sem, send_sem, recv_sem, ship_sem,
):
    freq = lax.axis_index("freq")
    tm = lax.axis_index("tm")
    tm_count = lax.axis_size("tm")
    z = lax.div(freq, 2)
    core = lax.rem(freq, 2)
    bits = [lax.rem(z, 2), lax.rem(lax.div(z, 2), 2), lax.div(z, 4)]
    partner = {"freq": freq + 1 - 2 * core}
    ring = ({"freq": lax.rem(freq + 2, 16)}, {"freq": lax.rem(freq + 14, 16)})
    flat = raw.reshape(2 * SET, 128)
    mine = pl.ds(core * 16, 16)

    def ahead(distance):
        return {"tm": lax.rem(tm + tm_count + distance, tm_count)}

    def tiles(first, count):
        return pl.ds((HERE + first) * 8, count * 8)

    own = pltpu.make_async_copy(x, raw.at[mine, tiles(0, 8), :], local_sem)
    own.start()
    tables = [
        pltpu.make_async_copy(source, target, table_sem.at[n])
        for n, (source, target) in enumerate(
            ((lower, lower_table), (upper, upper_table), (delays, delay_table), (counts, live))
        )
    ]
    for table in tables:
        table.start()

    barrier = pltpu.get_barrier_semaphore()
    peers = [partner, *ring, ahead(1), ahead(-1), ahead(2), ahead(-2)]
    for peer in peers:
        pl.semaphore_signal(barrier, inc=1, device_id=peer, device_id_type=MESH)
    pl.semaphore_wait(barrier, len(peers))

    own.wait()

    def remote(source, target, send, recv, device):
        return pltpu.make_async_remote_copy(
            src_ref=source, dst_ref=target, send_sem=send, recv_sem=recv,
            device_id=device, device_id_type=MESH,
        )

    def sends(distance):
        return tm < tm_count + distance if distance < 0 else tm >= 0

    def receives(distance):
        return tm >= -distance if distance < 0 else tm >= 0

    early = []
    for n, (distance, first, count) in enumerate(FETCHES[0]):
        place = raw.at[mine, tiles(distance * 8 + first, count), :]
        early.append((
            distance,
            remote(raw.at[mine, tiles(first, count), :], place, early_sem.at[4 * n], early_sem.at[4 * n + 1], ahead(-distance)),
            remote(place, place, early_sem.at[4 * n + 2], early_sem.at[4 * n + 3], partner),
        ))
    fetched = []
    for n, (phase, distance, first, count) in enumerate(LATE):
        place = late.at[n, mine, pl.ds(0, count * 8), :]
        fetched.append((
            phase, distance, distance * 8 + first, count,
            remote(raw.at[mine, tiles(first, count), :], place, late_sem.at[4 * n], late_sem.at[4 * n + 1], ahead(-distance)),
            remote(place, place, late_sem.at[4 * n + 2], late_sem.at[4 * n + 3], partner),
        ))
    to_partner = remote(
        raw.at[mine, tiles(0, 8), :], raw.at[mine, tiles(0, 8), :], own_sem.at[0], own_sem.at[1], partner
    )

    for distance, copy, _ in early:
        pl.when(sends(distance))(copy.start)
    for _, distance, _, _, copy, _ in fetched:
        pl.when(sends(distance))(copy.start)
    to_partner.start()

    def clear(base, first, count):
        def body(g, carry):
            raw[base + g, tiles(first, count), :] = jnp.zeros((count * 8, 128), jnp.float32)
            return carry
        lax.fori_loop(0, GROUPS, body, 0)

    raw[GROUPS, :, :] = jnp.zeros((SPAN, 128), jnp.float32)

    @pl.when(tm == 0)
    def _():
        clear(0, -10, 10)

    @pl.when(tm == 1)
    def _():
        clear(0, -10, 2)

    @pl.when(tm == tm_count - 1)
    def _():
        clear(GROUPS + 1, -HERE, HERE + 8)
        raw[2 * GROUPS + 1, :, :] = jnp.zeros((SPAN, 128), jnp.float32)

    for table in tables:
        table.wait()

    def entries(k, block):
        at = (pl.ds(k, 1), pl.ds(block, 128))
        row = jnp.where(bits[k] == 1, upper_table[at], lower_table[at])
        return row * 2048 + delay_table[at] * bits[k]

    def look_up(k, index):
        found = jnp.zeros((8, 128), jnp.int32)
        for block in range(DMAX // 128):
            table = jnp.broadcast_to(entries(k, block * 128), (8, 128))
            here = jnp.take_along_axis(table, index & 127, axis=1)
            found = jnp.where(index >> 7 == block, here, found)
        return found

    def is_live(k, index):
        bands = 4 >> k
        width = DMAX // bands
        first = 8 - (8 >> k)
        count = jnp.full((8, 128), live[first], jnp.int32)
        for band in range(1, bands):
            count = jnp.where(index // width == band, live[first + band], count)
        return (index & (width - 1)) < count

    for offset in range(CHIPS):
        block = lax.rem(z + offset, CHIPS) * 256 + core * ROWS
        packed[pl.ds(offset, 1), :] = entries(2, pl.multiple_of(block, 128))
    top = packed[...]
    middle = look_up(1, top >> 11)
    bottom = look_up(0, middle >> 11)
    delay = (top & 2047) + (middle & 2047) + (bottom & 2047)
    row = (bottom >> 11) & 255
    start = (row >> 3) * SPAN + (row & 7) + (HERE - (delay >> 7)) * 8
    start = jnp.where(is_live(1, top >> 11) & is_live(0, middle >> 11), start, ZERO_ROW + HERE * 8)
    packed[...] = start * 128 + (delay & 127)
    to_scalar = pltpu.make_async_copy(packed, picks, table_sem.at[0])
    to_scalar.start()
    to_scalar.wait()

    for distance, copy, across in early:
        @pl.when(receives(distance))
        def _(copy=copy, across=across):
            copy.wait_recv()
            across.start()
    to_partner.wait_recv()
    for distance, _, across in early:
        pl.when(receives(distance))(across.wait_recv)

    @pl.when(tm == tm_count - 1)
    def _():
        def body(g, carry):
            raw[GROUPS + 1 + g, tiles(8, SKEW), :] = raw[g, tiles(8, SKEW), :]
            return carry
        lax.fori_loop(0, GROUPS, body, 0)

    def forward(phase):
        for when, distance, _, _, copy, across in fetched:
            if when == phase:
                @pl.when(receives(distance))
                def _(copy=copy, across=across):
                    copy.wait_recv()
                    across.start()

    def settle(phase):
        for n, (when, distance, first, count, _, across) in enumerate(fetched):
            if when == phase:
                @pl.when(receives(distance))
                def _(n=n, first=first, count=count, across=across):
                    across.wait_recv()

                    def body(g, carry):
                        raw[g, tiles(first, count), :] = late[n, g, pl.ds(0, count * 8), :]
                        return carry
                    lax.fori_loop(0, GROUPS, body, 0)

    lanes = lax.broadcasted_iota(jnp.int32, (WIDTH, 128), 1)
    wrapped = jnp.where(tm == tm_count - 1, SET, 0)

    def first_tile(phase):
        return SKEW + 8 - (phase + 1) * WIDTH

    def contribution(phase, offset, row):
        entry = picks[offset, row]
        start = (entry >> 7) + first_tile(phase) * 8
        if first_tile(phase) >= 8:
            start = start + wrapped
        shift = entry & 127
        same = flat[pl.ds(start, WIDTH, stride=8), :]
        before = flat[pl.ds(start - 8, WIDTH, stride=8), :]
        return pltpu.roll(jnp.where(lanes < 128 - shift, same, before), shift, 1)

    def message(phase, direction, step, half, unit):
        return (((phase * 2 + direction) * 4 + step) * 2 + half) * HALF_UNITS + unit

    def copy_of(*entry):
        index = message(*entry)
        return remote(sent.at[index], landed.at[index], send_sem.at[index], recv_sem.at[index], ring[entry[1]])

    def add_and_send(phase, direction, step, half, unit):
        index = message(phase, direction, step, half, unit)
        offset = 4 - step if direction == 0 else 4 + step
        first_row = half * 64 + unit * UNIT
        fresh = step == 0 or (step == 1 and half != direction)
        previous = message(phase, direction, step - 1, half, unit)
        if not fresh:
            copy_of(phase, direction, step - 1, half, unit).wait_recv()

        def body(i, carry):
            for k in range(8):
                row = i * 8 + k
                value = contribution(phase, offset, first_row + row)
                at = pl.ds(pl.multiple_of(row * WIDTH, WIDTH), WIDTH)
                if not fresh:
                    value = value + landed[previous, at, :]
                sent[index, at, :] = value
            return carry

        lax.fori_loop(0, UNIT // 8, body, 0)
        copy_of(phase, direction, step, half, unit).start()

    def ship(phase, half, unit):
        index = (phase * 2 + half) * HALF_UNITS + unit
        return remote(shipped.at[index], received.at[index], ship_sem.at[0, index], ship_sem.at[1, index], ahead(1))

    def finish(phase, half, unit):
        incoming = []
        for direction in range(2):
            copy_of(phase, direction, 3, half, unit).wait_recv()
            incoming.append(message(phase, direction, 3, half, unit))
        first_row = half * 64 + unit * UNIT
        tile = first_tile(phase)
        index = (phase * 2 + half) * HALF_UNITS + unit

        def body(i, carry):
            for k in range(8):
                row = i * 8 + k
                at = pl.ds(pl.multiple_of(row * WIDTH, WIDTH), WIDTH)
                value = contribution(phase, 0, first_row + row)
                value = value + landed[incoming[0], at, :] + landed[incoming[1], at, :]
                alive = freq * ROWS + first_row + row < live[6]
                value = jnp.where(alive, value, jnp.zeros_like(value))
                if tile >= 8:
                    shipped[index, pl.ds(i * WIDTH * 8 + k, WIDTH, stride=8), :] = value
                else:
                    out[pl.ds(first_row * 8 + i * 64 + tile * 8 + k, WIDTH, stride=8), :] = value
            return carry

        lax.fori_loop(0, UNIT // 8, body, 0)
        if tile >= 8:
            ship(phase, half, unit).start()

    def take(phase, half, unit):
        ship(phase, half, unit).wait_recv()
        index = (phase * 2 + half) * HALF_UNITS + unit
        first = half * 64 + unit * UNIT
        tile = first_tile(phase) - 8
        for group in range(UNIT // 8):
            rows = pl.ds(group * WIDTH * 8, WIDTH * 8)
            out[pl.ds(first * 8 + group * 64 + tile * 8, WIDTH * 8), :] = received[index, rows, :]

    def exchange(phase, step, turn):
        for unit in range(HALF_UNITS):
            for direction in range(2):
                half = direction if turn == 1 else 1 - direction
                messages.append((phase, direction, step, half, unit))
                add_and_send(*messages[-1])

    parts = [(half, unit) for half in range(2) for unit in range(HALF_UNITS)]
    messages = []
    for phase in range(PHASES):
        if phase > 0:
            settle(phase)
        exchange(phase, 0, 1)
        exchange(phase, 1, 0)
        if phase > 0:
            for part in parts:
                finish(phase - 1, *part)
        exchange(phase, 1, 1)
        if phase + 1 < PHASES:
            forward(phase + 1)
        exchange(phase, 2, 0)
        exchange(phase, 2, 1)
        exchange(phase, 3, 0)
        exchange(phase, 3, 1)
    shipments = [(phase, *part) for phase in range(PHASES) if first_tile(phase) >= 8 for part in parts]
    for shipment in shipments:
        if shipment[0] < PHASES - 1:
            take(*shipment)
    for part in parts:
        finish(PHASES - 1, *part)

    for distance, copy, across in early:
        pl.when(sends(distance))(copy.wait_send)
        pl.when(receives(distance))(across.wait_send)
    for _, distance, _, _, copy, across in fetched:
        pl.when(sends(distance))(copy.wait_send)
        pl.when(receives(distance))(across.wait_send)
    to_partner.wait_send()
    for entry in messages:
        copy_of(*entry).wait_send()
    for shipment in shipments:
        ship(*shipment).wait_send()


def per_device(band_state, lower_rows, upper_rows, delays, counts):
    blocks = band_state.reshape(16, 8, 8, 128).transpose(0, 2, 1, 3).reshape(16, 64, 128)
    message_count = PHASES * 2 * 4 * 2 * HALF_UNITS
    part_count = PHASES * 2 * HALF_UNITS
    late_tiles = max(piece[3] for piece in LATE)
    operands = (blocks, lower_rows, upper_rows, delays, counts)
    dma = pltpu.SemaphoreType.DMA
    out = pl.pallas_call(
        kernel,
        out_shape=jax.ShapeDtypeStruct((1024, 128), jnp.float32),
        in_specs=[pl.BlockSpec(memory_space=pltpu.HBM)] * 5,
        out_specs=pl.BlockSpec(memory_space=pltpu.VMEM),
        scratch_shapes=[
            pltpu.VMEM((2 * (GROUPS + 1), SPAN, 128), jnp.float32),
            pltpu.VMEM((ITERS, DMAX), jnp.int32),
            pltpu.VMEM((ITERS, DMAX), jnp.int32),
            pltpu.VMEM((ITERS, DMAX), jnp.int32),
            pltpu.SMEM((7,), jnp.int32),
            pltpu.VMEM((CHIPS, ROWS), jnp.int32),
            pltpu.SMEM((CHIPS, ROWS), jnp.int32),
            pltpu.VMEM((message_count, UNIT * WIDTH, 128), jnp.float32),
            pltpu.VMEM((message_count, UNIT * WIDTH, 128), jnp.float32),
            pltpu.VMEM((len(LATE), GROUPS, late_tiles * 8, 128), jnp.float32),
            pltpu.VMEM((part_count, UNIT * WIDTH, 128), jnp.float32),
            pltpu.VMEM((part_count, UNIT * WIDTH, 128), jnp.float32),
            dma,
            dma((4,)),
            dma((2,)),
            dma((8,)),
            dma((4 * len(LATE),)),
            dma((message_count,)),
            dma((message_count,)),
            dma((2, part_count)),
        ],
        compiler_params=pltpu.CompilerParams(collective_id=0, has_side_effects=True, vmem_limit_bytes=48 << 20),
    )(*(pltpu.with_memory_space_constraint(operand, pltpu.HBM) for operand in operands))
    return out.reshape(16, 8, 8, 128).transpose(0, 2, 1, 3).reshape(ROWS, 1024)


def solution(mesh):
    return jax.shard_map(
        per_device,
        mesh=mesh,
        in_specs=(P("freq", "tm"), P(), P(), P(), P()),
        out_specs=P("freq", "tm"),
        check_vma=False,
    )
```

time: 76 us -> 66.5 us (0.88); the launches traced: 76 us -> 65.6 us
  Pallas kernels: 75.2 us -> 64.8 us
    pallas_call x1, Pallas kernels: 75.2 us -> 64.8 us  [per_device(): pl.pallas_call(kernel, out_shape=jax.ShapeDtypeStruct((1024, 128), jnp.fl...]
where the time goes in v3:
time: 66.5 us; the launch traced here: 65.6 us
  Pallas kernels  64.8 us (97%)
  local copies, waits for them, and re-layouts  0.8 us (1%)
    pallas_call x1, Pallas kernels, per_device(): pl.pallas_call(kernel, out_shape=jax.ShapeDtypeStruct((1024, 128), jnp.fl...  64.8 us

profile of v3, /device:TPU:5, one launch (start us, length us, event | category | flops | bytes accessed | tf_op | source)
XLA Modules:
  0.0 65.6 jit_solution(4794739871218202050)
XLA Ops:
  0.0 64.8 %shard_map.55 = f32[1024,128]{1,0:T(8,128)S(1)} custom-call(f32[16,64,128]{2,1,0:T(8,128)} %bitcast.11, s32[3,2048]{1,0:T(4,128)} %lower.1, s32[3,2048]{1,0:T(4,128)} %upper.1, s32[3,2048]{1,0:T(4,128)} %delays.1, s32[7]{0:T(128)} %counts.1), custom_call_target="tpu_custom_call" | custom-call | tf_op jit(solution)/shard_map/pallas_call | solution.py:352
  64.8 0.8 %copy.7 = f32[128,1024]{1,0:T(8,128)} copy(f32[128,1024]{1,0:T(8,128)S(1)} %bitcast.10) | data formatting | bytes 1048576

commit v4 on v3

--- a/solution.py
+++ b/solution.py
@@ -17,29 +17,24 @@
 SET = (GROUPS + 1) * SPAN
 HERE = 11
 SKEW = 4
-PHASES = 2
-WIDTH = 8 // PHASES
-UNIT = 32
-HALF_UNITS = 64 // UNIT
+UNIT = 64
+UNITS = ROWS // UNIT
+FINISH_ORDER = [unit + side * UNITS // 2 for unit in range(UNITS // 2) for side in range(2)]
 ZERO_ROW = GROUPS * SPAN
-
-EARLY = SKEW + 8 - WIDTH - 14
-FETCHES = [[(-1, 8 + EARLY, -EARLY), (1, 0, SKEW)]]
-for phase in range(1, PHASES):
-    last = EARLY - (phase - 1) * WIDTH
-    first = last - WIDTH
-    pieces = []
-    if last > -8:
-        pieces.append((-1, 8 + max(first, -8), last - max(first, -8)))
-    if first < -8:
-        pieces.append((-2, 16 + first, min(last, -8) - first))
-    FETCHES.append(pieces)
-LATE = [(phase, *piece) for phase in range(1, PHASES) for piece in FETCHES[phase]]
+PHASES = ((10, 2), (8, 2), (4, 4))
+PARTS = 1
+
+FETCHES = (((-1, 4, 4), (1, 0, 4)), ((-1, 2, 2),), ((-1, 0, 2), (-2, 6, 2)))
+LATE = tuple((phase, *piece) for phase in range(1, len(PHASES)) for piece in FETCHES[phase])
+LATE_TILES = max(piece[3] for piece in LATE)
+
+MESSAGE_ROWS = [sum(2 * 4 * ROWS * width for _, width in PHASES[:phase]) for phase in range(len(PHASES) + 1)]
+RESULT_ROWS = [sum(ROWS * width for _, width in PHASES[:phase]) for phase in range(len(PHASES) + 1)]
 
 
 def kernel(
     x, lower, upper, delays, counts, out,
-    raw, lower_table, upper_table, delay_table, live, packed, picks, sent, landed, late, shipped, received,
+    raw, lower_table, upper_table, delay_table, live, packed, picks, sent, landed, late, shipped, received, partial,
     local_sem, table_sem, own_sem, early_sem, late_sem, send_sem, recv_sem, ship_sem,
 ):
     freq = lax.axis_index("freq")
@@ -90,14 +85,19 @@
     def receives(distance):
         return tm >= -distance if distance < 0 else tm >= 0
 
+    size = 16 // PARTS
+    shares = [pl.ds(core * 16 + part * size, size) for part in range(PARTS)]
     early = []
-    for n, (distance, first, count) in enumerate(FETCHES[0]):
-        place = raw.at[mine, tiles(distance * 8 + first, count), :]
-        early.append((
-            distance,
-            remote(raw.at[mine, tiles(first, count), :], place, early_sem.at[4 * n], early_sem.at[4 * n + 1], ahead(-distance)),
-            remote(place, place, early_sem.at[4 * n + 2], early_sem.at[4 * n + 3], partner),
-        ))
+    for distance, first, count in FETCHES[0]:
+        for share in shares:
+            place = raw.at[share, tiles(distance * 8 + first, count), :]
+            n = 4 * len(early)
+            early.append((
+                distance,
+                remote(raw.at[share, tiles(first, count), :], place, early_sem.at[n], early_sem.at[n + 1], ahead(-distance)),
+                remote(place, place, early_sem.at[n + 2], early_sem.at[n + 3], partner),
+            ))
+    early = [entry for part in range(PARTS) for entry in early[part::PARTS]]
     fetched = []
     for n, (phase, distance, first, count) in enumerate(LATE):
         place = late.at[n, mine, pl.ds(0, count * 8), :]
@@ -213,121 +213,123 @@
                         return carry
                     lax.fori_loop(0, GROUPS, body, 0)
 
-    lanes = lax.broadcasted_iota(jnp.int32, (WIDTH, 128), 1)
     wrapped = jnp.where(tm == tm_count - 1, SET, 0)
 
-    def first_tile(phase):
-        return SKEW + 8 - (phase + 1) * WIDTH
-
     def contribution(phase, offset, row):
+        tile, width = PHASES[phase]
         entry = picks[offset, row]
-        start = (entry >> 7) + first_tile(phase) * 8
-        if first_tile(phase) >= 8:
+        start = (entry >> 7) + tile * 8
+        if tile >= 8:
             start = start + wrapped
         shift = entry & 127
-        same = flat[pl.ds(start, WIDTH, stride=8), :]
-        before = flat[pl.ds(start - 8, WIDTH, stride=8), :]
+        same = flat[pl.ds(start, width, stride=8), :]
+        before = flat[pl.ds(start - 8, width, stride=8), :]
+        lanes = lax.broadcasted_iota(jnp.int32, (width, 128), 1)
         return pltpu.roll(jnp.where(lanes < 128 - shift, same, before), shift, 1)
 
-    def message(phase, direction, step, half, unit):
-        return (((phase * 2 + direction) * 4 + step) * 2 + half) * HALF_UNITS + unit
-
-    def copy_of(*entry):
-        index = message(*entry)
-        return remote(sent.at[index], landed.at[index], send_sem.at[index], recv_sem.at[index], ring[entry[1]])
-
-    def add_and_send(phase, direction, step, half, unit):
-        index = message(phase, direction, step, half, unit)
+    def first_row(phase, direction, step, unit):
+        return MESSAGE_ROWS[phase] + ((direction * 4 + step) * UNITS + unit) * UNIT * PHASES[phase][1]
+
+    def copy_of(phase, direction, step, unit):
+        rows = pl.ds(first_row(phase, direction, step, unit), UNIT * PHASES[phase][1])
+        n = ((phase * 2 + direction) * 4 + step) * UNITS + unit
+        return remote(sent.at[rows, :], landed.at[rows, :], send_sem.at[n], recv_sem.at[n], ring[direction])
+
+    def is_long(direction, unit):
+        return (unit < UNITS // 2) == (direction == 0)
+
+    messages = []
+
+    def add_and_send(phase, direction, step, unit, fresh):
+        width = PHASES[phase][1]
         offset = 4 - step if direction == 0 else 4 + step
-        first_row = half * 64 + unit * UNIT
-        fresh = step == 0 or (step == 1 and half != direction)
-        previous = message(phase, direction, step - 1, half, unit)
+        target = first_row(phase, direction, step, unit)
+        source = first_row(phase, direction, step - 1, unit)
         if not fresh:
-            copy_of(phase, direction, step - 1, half, unit).wait_recv()
-
-        def body(i, carry):
-            for k in range(8):
-                row = i * 8 + k
-                value = contribution(phase, offset, first_row + row)
-                at = pl.ds(pl.multiple_of(row * WIDTH, WIDTH), WIDTH)
-                if not fresh:
-                    value = value + landed[previous, at, :]
-                sent[index, at, :] = value
-            return carry
-
-        lax.fori_loop(0, UNIT // 8, body, 0)
-        copy_of(phase, direction, step, half, unit).start()
-
-    def ship(phase, half, unit):
-        index = (phase * 2 + half) * HALF_UNITS + unit
-        return remote(shipped.at[index], received.at[index], ship_sem.at[0, index], ship_sem.at[1, index], ahead(1))
-
-    def finish(phase, half, unit):
-        incoming = []
-        for direction in range(2):
-            copy_of(phase, direction, 3, half, unit).wait_recv()
-            incoming.append(message(phase, direction, 3, half, unit))
-        first_row = half * 64 + unit * UNIT
-        tile = first_tile(phase)
-        index = (phase * 2 + half) * HALF_UNITS + unit
-
-        def body(i, carry):
-            for k in range(8):
-                row = i * 8 + k
-                at = pl.ds(pl.multiple_of(row * WIDTH, WIDTH), WIDTH)
-                value = contribution(phase, 0, first_row + row)
-                value = value + landed[incoming[0], at, :] + landed[incoming[1], at, :]
-                alive = freq * ROWS + first_row + row < live[6]
-                value = jnp.where(alive, value, jnp.zeros_like(value))
+            copy_of(phase, direction, step - 1, unit).wait_recv()
+
+        for row in range(UNIT):
+            value = contribution(phase, offset, unit * UNIT + row)
+            if not fresh:
+                value = value + landed[pl.ds(source + row * width, width), :]
+            sent[pl.ds(target + row * width, width), :] = value
+        copy_of(phase, direction, step, unit).start()
+        messages.append((phase, direction, step, unit))
+
+    def exchange(phase, step, long, fresh):
+        for unit in range(UNITS):
+            for direction in range(2):
+                if is_long(direction, unit) == long:
+                    add_and_send(phase, direction, step, unit, fresh)
+
+    def begin(phase):
+        exchange(phase, 0, True, True)
+        exchange(phase, 1, False, True)
+
+    def go_on(phase, step):
+        if step > 1:
+            exchange(phase, step, False, False)
+        exchange(phase, step, True, False)
+
+    def ship(phase, unit):
+        width = PHASES[phase][1]
+        rows = pl.ds(RESULT_ROWS[phase] + unit * UNIT * width, UNIT * width)
+        n = phase * UNITS + unit
+        return remote(shipped.at[rows, :], received.at[rows, :], ship_sem.at[0, n], ship_sem.at[1, n], ahead(1))
+
+    def finish(phase):
+        tile, width = PHASES[phase]
+        for unit in FINISH_ORDER:
+            sources = [first_row(phase, direction, 3, unit) for direction in range(2)]
+            last = 0 if is_long(0, unit) else 1
+            copy_of(phase, 1 - last, 3, unit).wait_recv()
+            for row in range(UNIT):
+                value = contribution(phase, 0, unit * UNIT + row)
+                value = value + landed[pl.ds(sources[1 - last] + row * width, width), :]
+                alive = freq * ROWS + unit * UNIT + row < live[6]
+                partial[pl.ds(row * width, width), :] = jnp.where(alive, value, jnp.zeros_like(value))
+            copy_of(phase, last, 3, unit).wait_recv()
+            for row in range(UNIT):
+                alive = freq * ROWS + unit * UNIT + row < live[6]
+                value = landed[pl.ds(sources[last] + row * width, width), :]
+                value = partial[pl.ds(row * width, width), :] + jnp.where(alive, value, jnp.zeros_like(value))
                 if tile >= 8:
-                    shipped[index, pl.ds(i * WIDTH * 8 + k, WIDTH, stride=8), :] = value
+                    at = RESULT_ROWS[phase] + unit * UNIT * width + (row // 8) * width * 8 + row % 8
+                    shipped[pl.ds(at, width, stride=8), :] = value
                 else:
-                    out[pl.ds(first_row * 8 + i * 64 + tile * 8 + k, WIDTH, stride=8), :] = value
-            return carry
-
-        lax.fori_loop(0, UNIT // 8, body, 0)
-        if tile >= 8:
-            ship(phase, half, unit).start()
-
-    def take(phase, half, unit):
-        ship(phase, half, unit).wait_recv()
-        index = (phase * 2 + half) * HALF_UNITS + unit
-        first = half * 64 + unit * UNIT
-        tile = first_tile(phase) - 8
-        for group in range(UNIT // 8):
-            rows = pl.ds(group * WIDTH * 8, WIDTH * 8)
-            out[pl.ds(first * 8 + group * 64 + tile * 8, WIDTH * 8), :] = received[index, rows, :]
-
-    def exchange(phase, step, turn):
-        for unit in range(HALF_UNITS):
-            for direction in range(2):
-                half = direction if turn == 1 else 1 - direction
-                messages.append((phase, direction, step, half, unit))
-                add_and_send(*messages[-1])
-
-    parts = [(half, unit) for half in range(2) for unit in range(HALF_UNITS)]
-    messages = []
-    for phase in range(PHASES):
-        if phase > 0:
-            settle(phase)
-        exchange(phase, 0, 1)
-        exchange(phase, 1, 0)
-        if phase > 0:
-            for part in parts:
-                finish(phase - 1, *part)
-        exchange(phase, 1, 1)
-        if phase + 1 < PHASES:
-            forward(phase + 1)
-        exchange(phase, 2, 0)
-        exchange(phase, 2, 1)
-        exchange(phase, 3, 0)
-        exchange(phase, 3, 1)
-    shipments = [(phase, *part) for phase in range(PHASES) if first_tile(phase) >= 8 for part in parts]
-    for shipment in shipments:
-        if shipment[0] < PHASES - 1:
-            take(*shipment)
-    for part in parts:
-        finish(PHASES - 1, *part)
+                    out[pl.ds((unit * UNIT + row - row % 8) * 8 + tile * 8 + row % 8, width, stride=8), :] = value
+            if tile >= 8:
+                ship(phase, unit).start()
+
+    def take(phase):
+        tile, width = PHASES[phase]
+        for unit in range(UNITS):
+            ship(phase, unit).wait_recv()
+            for group in range(UNIT // 8):
+                rows = pl.ds(RESULT_ROWS[phase] + (unit * UNIT + group * 8) * width, 8 * width)
+                out[pl.ds(unit * UNIT * 8 + group * 64 + (tile - 8) * 8, 8 * width), :] = received[rows, :]
+
+    begin(0)
+    forward(1)
+    settle(1)
+    begin(1)
+    go_on(0, 1)
+    go_on(1, 1)
+    forward(2)
+    go_on(0, 2)
+    go_on(1, 2)
+    go_on(0, 3)
+    settle(2)
+    begin(2)
+    go_on(1, 3)
+    finish(0)
+    go_on(2, 1)
+    finish(1)
+    go_on(2, 2)
+    take(0)
+    go_on(2, 3)
+    take(1)
+    finish(2)
 
     for distance, copy, across in early:
         pl.when(sends(distance))(copy.wait_send)
@@ -338,15 +340,15 @@
     to_partner.wait_send()
     for entry in messages:
         copy_of(*entry).wait_send()
-    for shipment in shipments:
-        ship(*shipment).wait_send()
+    for phase, (tile, _) in enumerate(PHASES):
+        if tile >= 8:
+            for unit in range(UNITS):
+                ship(phase, unit).wait_send()
 
 
 def per_device(band_state, lower_rows, upper_rows, delays, counts):
     blocks = band_state.reshape(16, 8, 8, 128).transpose(0, 2, 1, 3).reshape(16, 64, 128)
-    message_count = PHASES * 2 * 4 * 2 * HALF_UNITS
-    part_count = PHASES * 2 * HALF_UNITS
-    late_tiles = max(piece[3] for piece in LATE)
+    message_count = len(PHASES) * 2 * 4 * UNITS
     operands = (blocks, lower_rows, upper_rows, delays, counts)
     dma = pltpu.SemaphoreType.DMA
     out = pl.pallas_call(
@@ -362,19 +364,20 @@
             pltpu.SMEM((7,), jnp.int32),
             pltpu.VMEM((CHIPS, ROWS), jnp.int32),
             pltpu.SMEM((CHIPS, ROWS), jnp.int32),
-            pltpu.VMEM((message_count, UNIT * WIDTH, 128), jnp.float32),
-            pltpu.VMEM((message_count, UNIT * WIDTH, 128), jnp.float32),
-            pltpu.VMEM((len(LATE), GROUPS, late_tiles * 8, 128), jnp.float32),
-            pltpu.VMEM((part_count, UNIT * WIDTH, 128), jnp.float32),
-            pltpu.VMEM((part_count, UNIT * WIDTH, 128), jnp.float32),
+            pltpu.VMEM((MESSAGE_ROWS[-1], 128), jnp.float32),
+            pltpu.VMEM((MESSAGE_ROWS[-1], 128), jnp.float32),
+            pltpu.VMEM((len(LATE), GROUPS, LATE_TILES * 8, 128), jnp.float32),
+            pltpu.VMEM((RESULT_ROWS[-1], 128), jnp.float32),
+            pltpu.VMEM((RESULT_ROWS[-1], 128), jnp.float32),
+            pltpu.VMEM((UNIT * max(width for _, width in PHASES), 128), jnp.float32),
             dma,
             dma((4,)),
             dma((2,)),
-            dma((8,)),
+            dma((4 * PARTS * len(FETCHES[0]),)),
             dma((4 * len(LATE),)),
             dma((message_count,)),
             dma((message_count,)),
-            dma((2, part_count)),
+            dma((2, len(PHASES) * UNITS)),
         ],
         compiler_params=pltpu.CompilerParams(collective_id=0, has_side_effects=True, vmem_limit_bytes=48 << 20),
     )(*(pltpu.with_memory_space_constraint(operand, pltpu.HBM) for operand in operands))

time: 66.5 us -> 63.7 us (0.958)
  the two profiles are of different devices: /device:TPU:5 before, /device:TPU:2 now
where the time goes in v4:
time: 63.7 us; the launch traced here: 63.6 us
  Pallas kernels  62.8 us (99%)
  local copies, waits for them, and re-layouts  0.8 us (1%)
    pallas_call x1, Pallas kernels, per_device(): pl.pallas_call(kernel, out_shape=jax.ShapeDtypeStruct((1024, 128), jnp.fl...  62.8 us

profile of v4, /device:TPU:2, one launch (start us, length us, event | category | flops | bytes accessed | tf_op | source)
XLA Modules:
  0.0 63.6 jit_solution(9768583536942697981)
XLA Ops:
  0.0 62.8 %shard_map.55 = f32[1024,128]{1,0:T(8,128)S(1)} custom-call(f32[16,64,128]{2,1,0:T(8,128)} %bitcast.11, s32[3,2048]{1,0:T(4,128)} %lower.1, s32[3,2048]{1,0:T(4,128)} %upper.1, s32[3,2048]{1,0:T(4,128)} %delays.1, s32[7]{0:T(128)} %counts.1), custom_call_target="tpu_custom_call" | custom-call | tf_op jit(solution)/shard_map/pallas_call | solution.py:354
  62.8 0.8 %copy.7 = f32[128,1024]{1,0:T(8,128)} copy(f32[128,1024]{1,0:T(8,128)S(1)} %bitcast.10) | data formatting | bytes 1048576

commit v5 on v4

--- a/solution.py
+++ b/solution.py
@@ -84,6 +84,9 @@
 
     def receives(distance):
         return tm >= -distance if distance < 0 else tm >= 0
+
+    def first_chip(phase, tile):
+        return (PHASES[phase][0] - tile) // 2 + 1
 
     size = 16 // PARTS
     shares = [pl.ds(core * 16 + part * size, size) for part in range(PARTS)]
@@ -110,10 +113,16 @@
         raw.at[mine, tiles(0, 8), :], raw.at[mine, tiles(0, 8), :], own_sem.at[0], own_sem.at[1], partner
     )
 
+    def reads_early(distance):
+        return z >= first_chip(len(PHASES) - 1, 0) if distance < 0 else z >= 0
+
     for distance, copy, _ in early:
-        pl.when(sends(distance))(copy.start)
-    for _, distance, _, _, copy, _ in fetched:
-        pl.when(sends(distance))(copy.start)
+        pl.when(sends(distance) & reads_early(distance))(copy.start)
+    def is_needed(first, count):
+        return z >= first_chip(len(PHASES) - 1, first + count)
+
+    for _, distance, first, count, copy, _ in fetched:
+        pl.when(sends(distance) & is_needed(first, count))(copy.start)
     to_partner.start()
 
     def clear(base, first, count):
@@ -178,13 +187,13 @@
     to_scalar.wait()
 
     for distance, copy, across in early:
-        @pl.when(receives(distance))
+        @pl.when(receives(distance) & reads_early(distance))
         def _(copy=copy, across=across):
             copy.wait_recv()
             across.start()
     to_partner.wait_recv()
     for distance, _, across in early:
-        pl.when(receives(distance))(across.wait_recv)
+        pl.when(receives(distance) & reads_early(distance))(across.wait_recv)
 
     @pl.when(tm == tm_count - 1)
     def _():
@@ -193,18 +202,22 @@
             return carry
         lax.fori_loop(0, GROUPS, body, 0)
 
+    def when_first_read(phase, distance, first, count):
+        here = receives(distance) & (z >= first_chip(phase, first + count))
+        return here & (z < first_chip(phase - 1, first + count)) if phase > 1 else here
+
     def forward(phase):
-        for when, distance, _, _, copy, across in fetched:
-            if when == phase:
-                @pl.when(receives(distance))
+        for when, distance, first, count, copy, across in fetched:
+            if when <= phase:
+                @pl.when(when_first_read(phase, distance, first, count))
                 def _(copy=copy, across=across):
                     copy.wait_recv()
                     across.start()
 
     def settle(phase):
         for n, (when, distance, first, count, _, across) in enumerate(fetched):
-            if when == phase:
-                @pl.when(receives(distance))
+            if when <= phase:
+                @pl.when(when_first_read(phase, distance, first, count))
                 def _(n=n, first=first, count=count, across=across):
                     across.wait_recv()
 
@@ -315,15 +328,16 @@
     begin(1)
     go_on(0, 1)
     go_on(1, 1)
+    go_on(0, 2)
     forward(2)
-    go_on(0, 2)
     go_on(1, 2)
+    settle(2)
+    exchange(2, 0, True, True)
     go_on(0, 3)
-    settle(2)
-    begin(2)
+    exchange(2, 1, False, True)
     go_on(1, 3)
+    go_on(2, 1)
     finish(0)
-    go_on(2, 1)
     finish(1)
     go_on(2, 2)
     take(0)
@@ -332,11 +346,11 @@
     finish(2)
 
     for distance, copy, across in early:
-        pl.when(sends(distance))(copy.wait_send)
-        pl.when(receives(distance))(across.wait_send)
-    for _, distance, _, _, copy, across in fetched:
-        pl.when(sends(distance))(copy.wait_send)
-        pl.when(receives(distance))(across.wait_send)
+        pl.when(sends(distance) & reads_early(distance))(copy.wait_send)
+        pl.when(receives(distance) & reads_early(distance))(across.wait_send)
+    for _, distance, first, count, copy, across in fetched:
+        pl.when(sends(distance) & is_needed(first, count))(copy.wait_send)
+        pl.when(receives(distance) & is_needed(first, count))(across.wait_send)
     to_partner.wait_send()
     for entry in messages:
         copy_of(*entry).wait_send()

time: 63.7 us -> 63.5 us (level)
  the two profiles are of different devices: /device:TPU:2 before, /device:TPU:5 now
where the time goes in v5:
time: 63.5 us; the launch traced here: 62.2 us
  Pallas kernels  61.4 us (97%)
  local copies, waits for them, and re-layouts  0.8 us (1%)
    pallas_call x1, Pallas kernels, per_device(): pl.pallas_call(kernel, out_shape=jax.ShapeDtypeStruct((1024, 128), jnp.fl...  61.4 us

profile of v5, /device:TPU:5, one launch (start us, length us, event | category | flops | bytes accessed | tf_op | source)
XLA Modules:
  0.0 62.2 jit_solution(10080231967386228812)
XLA Ops:
  0.0 61.4 %shard_map.55 = f32[1024,128]{1,0:T(8,128)S(1)} custom-call(f32[16,64,128]{2,1,0:T(8,128)} %bitcast.11, s32[3,2048]{1,0:T(4,128)} %lower.1, s32[3,2048]{1,0:T(4,128)} %upper.1, s32[3,2048]{1,0:T(4,128)} %delays.1, s32[7]{0:T(128)} %counts.1), custom_call_target="tpu_custom_call" | custom-call | tf_op jit(solution)/shard_map/pallas_call | solution.py:368
  61.5 0.8 %copy.7 = f32[128,1024]{1,0:T(8,128)} copy(f32[128,1024]{1,0:T(8,128)S(1)} %bitcast.10) | data formatting | bytes 1048576

commit v6 on v5

--- a/solution.py
+++ b/solution.py
@@ -325,8 +325,9 @@
     begin(0)
     forward(1)
     settle(1)
-    begin(1)
+    exchange(1, 0, True, True)
     go_on(0, 1)
+    exchange(1, 1, False, True)
     go_on(1, 1)
     go_on(0, 2)
     forward(2)

time: 63.5 us -> 63.5 us (level)
  no operation moved by 1% of the time
where the time goes in v6:
time: 63.5 us; the launch traced here: 62.3 us
  Pallas kernels  61.4 us (97%)
  local copies, waits for them, and re-layouts  0.8 us (1%)
    pallas_call x1, Pallas kernels, per_device(): pl.pallas_call(kernel, out_shape=jax.ShapeDtypeStruct((1024, 128), jnp.fl...  61.4 us

profile of v6, /device:TPU:5, one launch (start us, length us, event | category | flops | bytes accessed | tf_op | source)
XLA Modules:
  0.0 62.3 jit_solution(17715244990589189750)
XLA Ops:
  0.0 61.4 %shard_map.55 = f32[1024,128]{1,0:T(8,128)S(1)} custom-call(f32[16,64,128]{2,1,0:T(8,128)} %bitcast.11, s32[3,2048]{1,0:T(4,128)} %lower.1, s32[3,2048]{1,0:T(4,128)} %upper.1, s32[3,2048]{1,0:T(4,128)} %delays.1, s32[7]{0:T(128)} %counts.1), custom_call_target="tpu_custom_call" | custom-call | tf_op jit(solution)/shard_map/pallas_call | solution.py:369
  61.5 0.8 %copy.7 = f32[128,1024]{1,0:T(8,128)} copy(f32[128,1024]{1,0:T(8,128)S(1)} %bitcast.10) | data formatting | bytes 1048576

commit v7 on v5

--- a/solution.py
+++ b/solution.py
@@ -121,8 +121,12 @@
     def is_needed(first, count):
         return z >= first_chip(len(PHASES) - 1, first + count)
 
-    for _, distance, first, count, copy, _ in fetched:
-        pl.when(sends(distance) & is_needed(first, count))(copy.start)
+    def request(phase):
+        for when, distance, first, count, copy, _ in fetched:
+            if when == phase:
+                pl.when(sends(distance) & is_needed(first, count))(copy.start)
+
+    request(1)
     to_partner.start()
 
     def clear(base, first, count):
@@ -326,6 +330,7 @@
     forward(1)
     settle(1)
     begin(1)
+    request(2)
     go_on(0, 1)
     go_on(1, 1)
     go_on(0, 2)

time: 63.5 us -> 63.3 us (level)
  the two profiles are of different devices: /device:TPU:5 before, /device:TPU:3 now
where the time goes in v7:
time: 63.3 us; the launch traced here: 63.2 us
  Pallas kernels  62.4 us (99%)
  local copies, waits for them, and re-layouts  0.8 us (1%)
    pallas_call x1, Pallas kernels, per_device(): pl.pallas_call(kernel, out_shape=jax.ShapeDtypeStruct((1024, 128), jnp.fl...  62.4 us

profile of v7, /device:TPU:3, one launch (start us, length us, event | category | flops | bytes accessed | tf_op | source)
XLA Modules:
  0.0 63.2 jit_solution(6430724898089770044)
XLA Ops:
  0.0 62.4 %shard_map.55 = f32[1024,128]{1,0:T(8,128)S(1)} custom-call(f32[16,64,128]{2,1,0:T(8,128)} %bitcast.11, s32[3,2048]{1,0:T(4,128)} %lower.1, s32[3,2048]{1,0:T(4,128)} %upper.1, s32[3,2048]{1,0:T(4,128)} %delays.1, s32[7]{0:T(128)} %counts.1), custom_call_target="tpu_custom_call" | custom-call | tf_op jit(solution)/shard_map/pallas_call | solution.py:373
  62.4 0.8 %copy.7 = f32[128,1024]{1,0:T(8,128)} copy(f32[128,1024]{1,0:T(8,128)S(1)} %bitcast.10) | data formatting | bytes 1048576
